TPU v7x, 32 devices: a whole 2x2x4 slice. The times are simulated.
32 devices in a mesh: row: 4 (over y, x), col: 8 (over z, core).
Axes of the slice: x: 2, y: 2, z: 4, core: 2. Of those that a mesh axis runs over, the one named last changes fastest.
Arguments:
- features: bfloat16 [8192, 512], P(('row', 'col')), may hold values from -6 to 6
- tile_values: bfloat16 [4, 8, 128, 128, 128], P('row', 'col'), may hold values from -0.1875 to 0.1875
- tile_places: int32 [4, 8, 2, 128], P('row', 'col'), may hold values from 0 to 15, as said below
- tile_counts: int32 [4, 8], replicated, may hold values from 40 to 128, as said below
- weight_one: float32 [512, 512], replicated, may hold values from -0.25 to 0.25
- weight_two: float32 [512, 512], replicated, may hold values from -0.25 to 0.25
Outputs:
- embedded: float32 [8192, 512], P(('row', 'col'))
Inputs may be any that keep to these rules, and one draw needn't show every extreme that they name: `tile_places`: in every block the first tile_counts slots name distinct tiles with tile rows below 16 and tile columns below 8, listed in order of tile row (never falling); later slots also name tiles in range. `tile_counts`: some block has exactly 128 tiles.
All inputs are finite; a program needn't handle non-finite values.
Results may differ from a plain program's by a relative error of at most 0.0029.
Values may be sent and summed in bfloat16 or wider, within the bound.
A program may use at most 64 MiB of HBM per device.

v0:
```python
import jax
import jax.numpy as jnp
from jax import lax
from jax.sharding import PartitionSpec as P

TR = 16


def add_slots(
    partial_value, blocks, row_ids, col_ids, column_tiles, first_slot, stop_slot, row_base
):
    slot_count = blocks.shape[0]
    group_size = min(16, slot_count)
    last_row = partial_value.shape[0] - 1

    def one_turn(group, totals):
        offset = jnp.minimum(group * group_size, slot_count - group_size)
        tile_group = lax.dynamic_slice_in_dim(blocks, offset, group_size, 0)
        group_rows = lax.dynamic_slice_in_dim(row_ids, offset, group_size, 0)
        group_cols = lax.dynamic_slice_in_dim(col_ids, offset, group_size, 0)
        positions = offset + jnp.arange(group_size, dtype=jnp.int32)
        active = (positions >= jnp.maximum(first_slot, group * group_size)) & (
            positions < stop_slot
        )
        products = jnp.einsum(
            "sij,sjf->sif", tile_group, column_tiles[group_cols], preferred_element_type=jnp.float32
        )
        products = jnp.where(active[:, None, None], products, 0.0)
        local_rows = jnp.clip(group_rows - row_base, 0, last_row)
        return totals.at[local_rows].add(products)

    first_turn = first_slot // group_size
    last_turn = (stop_slot + group_size - 1) // group_size
    return lax.fori_loop(first_turn, last_turn, one_turn, partial_value)


def shards(features, tile_values, tile_places, tile_counts, weight_one, weight_two):
    blocks = tile_values.reshape(tile_values.shape[2:])
    places = tile_places.reshape(tile_places.shape[2:])
    tile_size = blocks.shape[1]
    width_all = features.shape[1]
    block_row = lax.axis_index("row")
    block_col = lax.axis_index("col")
    own_count = tile_counts[block_row, block_col]

    def layer(inputs, weights):
        gathered = lax.all_gather(inputs, "row", axis=0, tiled=True)
        column_tiles = gathered.reshape(gathered.shape[0] // tile_size, tile_size, width_all)
        partial_value = jnp.zeros((TR, tile_size, width_all), jnp.float32)
        partial_value = add_slots(
            partial_value, blocks, places[0], places[1], column_tiles, 0, own_count, 0
        )
        mine = lax.psum_scatter(
            partial_value.reshape(TR * tile_size, width_all), "col", scatter_dimension=0, tiled=True
        )
        return jnp.maximum(jnp.dot(mine, weights, precision=lax.Precision.HIGHEST), 0.0)

    hidden = layer(features, weight_one).astype(jnp.bfloat16)
    return layer(hidden, weight_two)


def solution(mesh):
    placed = (
        P(("row", "col"), None),
        P("row", "col", None, None, None),
        P("row", "col", None, None),
        P(),
        P(),
        P(),
    )
    return jax.shard_map(
        shards, mesh=mesh, in_specs=placed, out_specs=P(("row", "col"), None), check_vma=False
    )
```

profile of v0, /device:TPU:0, one launch (start us, length us, event | category | flops | bytes accessed | tf_op | source)
XLA Modules:
  0.0 430.2 jit_solution(628005692319676586)
XLA Ops:
  10.1 28.3 %all-gather.3.cloned.1.call-done = bf16[1024,512]{1,0:T(8,128)(2,1)} async-done(((bf16[256,512]{1,0:T(8,128)(2,1)}), bf16[1024,512]{1,0:T(8,128)(2,1)}) %all-gather.3.cloned.1.call-update) | async-done | bytes 1048592 | tf_op jit(solution)/shard_map/all_gather | solution.py:47
  38.4 2.5 broadcast.45.clone
  41.0 76.5 %while.20 = (s32[]{:T(128)}, f32[16,128,512]{2,1,0:T(8,128)}, s32[]{:T(128)}, s32[128]{0:T(128)S(1)}, s32[]{:T(128)}, /*index=5*/bf16[128,128,128]{2,1,0:T(8,128...) while((s32[]{:T(128)}, f32[16,128,512]{2,1,0:T(8,128)}, ...), condition=%wide.region_2.3_spmd, body=%wide.region_0.2_spmd.sunk | while | flops 270533824 | bytes 23597752 | solution.py:34
  41.0 1.9 gather_fusion
  43.7 3.7 convolution_select_fusion.4
  47.3 8.8 %scatter_fusion = f32[16,128,512]{2,1,0:T(8,128)} fusion(f32[16,128,512]{2,1,0:T(8,128)} %get-tuple-element.253, s32[16]{0:T(128)S(1)} %get-tuple-element.227, f32[16,128,512]{2,1,0:T(8,128)} %convolution_select_fusion.4), kind=kCustom, calls=%fused_computation.2.clone.1 | custom fusion | flops 1048576 | bytes 12582976 | tf_op jit(solution)/shard_map/while/body/scatter-add | solution.py:30
  58.9 3.7 convolution_select_fusion.4
  62.5 8.8 %scatter_fusion = f32[16,128,512]{2,1,0:T(8,128)} fusion(f32[16,128,512]{2,1,0:T(8,128)} %get-tuple-element.253, s32[16]{0:T(128)S(1)} %get-tuple-element.227, f32[16,128,512]{2,1,0:T(8,128)} %convolution_select_fusion.4), kind=kCustom, calls=%fused_computation.2.clone.1 | custom fusion | flops 1048576 | bytes 12582976 | tf_op jit(solution)/shard_map/while/body/scatter-add | solution.py:30
  74.1 3.7 convolution_select_fusion.4
  77.8 8.9 %scatter_fusion = f32[16,128,512]{2,1,0:T(8,128)} fusion(f32[16,128,512]{2,1,0:T(8,128)} %get-tuple-element.253, s32[16]{0:T(128)S(1)} %get-tuple-element.227, f32[16,128,512]{2,1,0:T(8,128)} %convolution_select_fusion.4), kind=kCustom, calls=%fused_computation.2.clone.1 | custom fusion | flops 1048576 | bytes 12582976 | tf_op jit(solution)/shard_map/while/body/scatter-add | solution.py:30
  86.8 1.9 gather_fusion
  89.4 3.7 convolution_select_fusion.4
  93.1 8.9 %scatter_fusion = f32[16,128,512]{2,1,0:T(8,128)} fusion(f32[16,128,512]{2,1,0:T(8,128)} %get-tuple-element.253, s32[16]{0:T(128)S(1)} %get-tuple-element.227, f32[16,128,512]{2,1,0:T(8,128)} %convolution_select_fusion.4), kind=kCustom, calls=%fused_computation.2.clone.1 | custom fusion | flops 1048576 | bytes 12582976 | tf_op jit(solution)/shard_map/while/body/scatter-add | solution.py:30
  104.7 3.7 convolution_select_fusion.4
  108.4 9.1 %scatter_fusion = f32[16,128,512]{2,1,0:T(8,128)} fusion(f32[16,128,512]{2,1,0:T(8,128)} %get-tuple-element.253, s32[16]{0:T(128)S(1)} %get-tuple-element.227, f32[16,128,512]{2,1,0:T(8,128)} %convolution_select_fusion.4), kind=kCustom, calls=%fused_computation.2.clone.1 | custom fusion | flops 1048576 | bytes 12582976 | tf_op jit(solution)/shard_map/while/body/scatter-add | solution.py:30
  117.5 98.0 %reduce-scatter.3.cloned.1.call-done = f32[256,512]{1,0:T(8,128)} async-done(((f32[2048,512]{1,0:T(8,128)}), f32[256,512]{1,0:T(8,128)}) %reduce-scatter.3.cloned.1.call-update) | async-done | bytes 524304 | tf_op jit(solution)/shard_map/reduce_scatter | solution.py:53
  215.5 2.8 fusion.4
  218.4 25.1 %all-gather.5.cloned.1.call-done = bf16[1024,512]{1,0:T(8,128)(2,1)} async-done(((bf16[256,512]{1,0:T(8,128)(2,1)}), bf16[1024,512]{1,0:T(8,128)(2,1)}) %all-gather.5.cloned.1.call-update) | async-done | bytes 1048592 | tf_op jit(solution)/shard_map/all_gather | solution.py:47
  243.5 2.5 broadcast.45
  245.9 76.8 %while.21 = (s32[]{:T(128)}, f32[16,128,512]{2,1,0:T(8,128)}, s32[]{:T(128)}, s32[128]{0:T(128)S(1)}, s32[]{:T(128)}, /*index=5*/bf16[128,128,128]{2,1,0:T(8,128...) while((s32[]{:T(128)}, f32[16,128,512]{2,1,0:T(8,128)}, ...), condition=%wide.region_6.7_spmd, body=%wide.region_4.6_spmd.sunk | while | flops 270533824 | bytes 23597752 | solution.py:34
  248.6 3.7 convolution_select_fusion.5
  252.4 9.1 %scatter_fusion.1 = f32[16,128,512]{2,1,0:T(8,128)} fusion(f32[16,128,512]{2,1,0:T(8,128)} %get-tuple-element.292, s32[16]{0:T(128)S(1)} %get-tuple-element.237, f32[16,128,512]{2,1,0:T(8,128)} %convolution_select_fusion.5), kind=kCustom, calls=%fused_computation.3.clone.1 | custom fusion | flops 1048576 | bytes 12582976 | tf_op jit(solution)/shard_map/while/body/scatter-add | solution.py:30
  264.1 3.7 convolution_select_fusion.5
  267.9 8.8 %scatter_fusion.1 = f32[16,128,512]{2,1,0:T(8,128)} fusion(f32[16,128,512]{2,1,0:T(8,128)} %get-tuple-element.292, s32[16]{0:T(128)S(1)} %get-tuple-element.237, f32[16,128,512]{2,1,0:T(8,128)} %convolution_select_fusion.5), kind=kCustom, calls=%fused_computation.3.clone.1 | custom fusion | flops 1048576 | bytes 12582976 | tf_op jit(solution)/shard_map/while/body/scatter-add | solution.py:30
  279.4 3.7 convolution_select_fusion.5
  283.1 8.8 %scatter_fusion.1 = f32[16,128,512]{2,1,0:T(8,128)} fusion(f32[16,128,512]{2,1,0:T(8,128)} %get-tuple-element.292, s32[16]{0:T(128)S(1)} %get-tuple-element.237, f32[16,128,512]{2,1,0:T(8,128)} %convolution_select_fusion.5), kind=kCustom, calls=%fused_computation.3.clone.1 | custom fusion | flops 1048576 | bytes 12582976 | tf_op jit(solution)/shard_map/while/body/scatter-add | solution.py:30
  294.7 3.7 convolution_select_fusion.5
  298.4 9.1 %scatter_fusion.1 = f32[16,128,512]{2,1,0:T(8,128)} fusion(f32[16,128,512]{2,1,0:T(8,128)} %get-tuple-element.292, s32[16]{0:T(128)S(1)} %get-tuple-element.237, f32[16,128,512]{2,1,0:T(8,128)} %convolution_select_fusion.5), kind=kCustom, calls=%fused_computation.3.clone.1 | custom fusion | flops 1048576 | bytes 12582976 | tf_op jit(solution)/shard_map/while/body/scatter-add | solution.py:30
  310.2 3.7 convolution_select_fusion.5
  313.9 8.8 %scatter_fusion.1 = f32[16,128,512]{2,1,0:T(8,128)} fusion(f32[16,128,512]{2,1,0:T(8,128)} %get-tuple-element.292, s32[16]{0:T(128)S(1)} %get-tuple-element.237, f32[16,128,512]{2,1,0:T(8,128)} %convolution_select_fusion.5), kind=kCustom, calls=%fused_computation.3.clone.1 | custom fusion | flops 1048576 | bytes 12582976 | tf_op jit(solution)/shard_map/while/body/scatter-add | solution.py:30
  322.7 98.0 %reduce-scatter.5.cloned.1.call-done = f32[256,512]{1,0:T(8,128)} async-done(((f32[2048,512]{1,0:T(8,128)}), f32[256,512]{1,0:T(8,128)}) %reduce-scatter.5.cloned.1.call-update) | async-done | bytes 524304 | tf_op jit(solution)/shard_map/reduce_scatter | solution.py:53
  420.8 2.9 convolution_maximum_fusion
  (52 shorter events, 26.0 us)
Async XLA Ops:
  6.5 209.0 %copy-start = (f32[512,512]{1,0:T(8,128)S(1)}, f32[512,512]{1,0:T(8,128)}, u32[]{:S(2)}) copy-start(f32[512,512]{1,0:T(8,128)} %param.14) | copy-start | bytes 3145732
  6.5 31.9 %all-gather.3.cloned.1.call-start = ((), (), s32[]{:S(2)}) async-start(), calls=%async_computation.2 | async-start | bytes 1310720 | tf_op jit(solution)/shard_map/all_gather | solution.py:47
  7.3 208.3 %reduce-scatter.3.cloned.1.call-start = ((), (), s32[]{:S(2)}) async-start(), calls=%async_computation.3 | async-start | bytes 4718592 | tf_op jit(solution)/shard_map/reduce_scatter | solution.py:53
  117.5 126.0 %all-gather.5.cloned.1.call-start = ((), (), s32[]{:S(2)}) async-start(), calls=%async_computation.4 | async-start | bytes 1310720 | tf_op jit(solution)/shard_map/all_gather | solution.py:47
  218.3 202.4 %reduce-scatter.5.cloned.1.call-start = ((), (), s32[]{:S(2)}) async-start(), calls=%async_computation.5 | async-start | bytes 4718592 | tf_op jit(solution)/shard_map/reduce_scatter | solution.py:53
  322.7 98.1 %copy-start.1 = (f32[512,512]{1,0:T(8,128)S(1)}, f32[512,512]{1,0:T(8,128)}, u32[]{:S(2)}) copy-start(f32[512,512]{1,0:T(8,128)} %param.15) | copy-start | bytes 3145732
Sparse Core Ops, SparseCore 0:
  9.2 29.2 all-gather.2
  117.6 97.8 reduce-scatter.2
  218.5 24.9 all-gather.4
  322.8 97.8 reduce-scatter.4
where the time goes:
time: 432 us; the launch traced here: 430 us
  waiting for transfers between devices  250 us (58%)
  other arithmetic  97 us (22%)
  matrix products  42.7 us (10%)
  local copies, waits for them, and re-layouts  26.2 us (6%)
  between operations  13.9 us (3%)
    reduce_scatter x2, waiting for transfers between devices, layer(): lax.psum_scatter(partial_value.reshape(TR * tile_size, width_all), 'col',...  196 us
    scatter-add x10, other arithmetic, one_turn(): return totals.at[local_rows].add(products)  89.2 us
    all_gather x2, waiting for transfers between devices, layer(): gathered = lax.all_gather(inputs, 'row', axis=0, tiled=True)  53.4 us
    dot_general x10, matrix products, one_turn(): jnp.einsum('sij,sjf->sif', tile_group, column_tiles[group_cols], preferre...  37.1 us
    gather x10, local copies, waits for them, and re-layouts, one_turn(): column_tiles[group_cols]  19.1 us
  transfers between devices with their start and end apart: 4, of which 4 were waited for; matrix products, arithmetic and copies ran while one was open for 0% of the time, Pallas kernels for 0%

commit v1 on v0

v1 whole, which is shorter than its diff:
```python
import functools

import jax
import jax.numpy as jnp
from jax import lax
from jax.experimental import pallas as pl
from jax.experimental.pallas import tpu as pltpu
from jax.sharding import PartitionSpec as P

MESH = pl.DeviceIdType.MESH
PARTS = 2
LINK_TYPES = (jnp.float32, jnp.bfloat16)


def kernel(
    n_row, n_col,
    inverse_ref, features_ref, tiles_hbm, weight_one_hbm, weight_two_hbm,
    out_ref,
    tiles, dense, weights, hidden, inputs, own, total,
    pair_out, pair_in, up_out0, up_in0, down_out0, down_in0, up_out1, up_in1, down_out1, down_in1,
    load_sem, gather_send, gather_recv, pair_send, pair_recv, up_send, up_recv, down_send, down_recv,
):
    row, col = lax.axis_index("row"), lax.axis_index("col")
    n_chip = n_col // 2
    chip, core = col // 2, col % 2
    partner = chip * 2 + (1 - core)
    slots, tile = tiles_hbm.shape[0], tiles_hbm.shape[1]
    piece, width = features_ref.shape
    part = width // PARTS
    tile_rows, tile_cols = dense.shape[0] // tile, dense.shape[1] // tile

    tile_load = pltpu.make_async_copy(tiles_hbm, tiles.at[pl.ds(0, slots)], load_sem.at[0])
    tile_load.start()
    weight_loads = [
        pltpu.make_async_copy(weight_one_hbm, weights.at[0], load_sem.at[1]),
        pltpu.make_async_copy(weight_two_hbm, weights.at[1], load_sem.at[2]),
    ]
    for load in weight_loads:
        load.start()

    barrier = pltpu.get_barrier_semaphore()
    for step in range(1, n_row):
        pl.semaphore_signal(
            barrier, inc=1, device_id=(lax.rem(row + step, n_row), col), device_id_type=MESH
        )
    pl.semaphore_signal(barrier, inc=1, device_id=(row, partner), device_id_type=MESH)

    @pl.when(chip > 0)
    def _():
        pl.semaphore_signal(barrier, inc=1, device_id=(row, col - 2), device_id_type=MESH)

    @pl.when(chip < n_chip - 1)
    def _():
        pl.semaphore_signal(barrier, inc=1, device_id=(row, col + 2), device_id_type=MESH)

    peers = n_row + jnp.where(chip > 0, 1, 0) + jnp.where(chip < n_chip - 1, 1, 0)
    pl.semaphore_wait(barrier, peers)

    def gather_copy(layer, source, h, step):
        return pltpu.make_async_remote_copy(
            src_ref=source.at[:, pl.ds(h * part, part)],
            dst_ref=inputs.at[layer, h, pl.ds(pl.multiple_of(row * piece, piece), piece), :],
            send_sem=gather_send.at[layer, h, step - 1],
            recv_sem=gather_recv.at[layer, h, step - 1],
            device_id=(lax.rem(row + step, n_row), col),
            device_id_type=MESH,
        )

    def pair_copy(layer, h, d):
        return pltpu.make_async_remote_copy(
            src_ref=pair_out.at[layer, h, d],
            dst_ref=pair_in.at[layer, h, d],
            send_sem=pair_send.at[layer, h, d],
            recv_sem=pair_recv.at[layer, h, d],
            device_id=(row, partner),
            device_id_type=MESH,
        )

    ups = ((up_out0, up_in0), (up_out1, up_in1))
    downs = ((down_out0, down_in0), (down_out1, down_in1))

    def up_copy(layer, h, j):
        return pltpu.make_async_remote_copy(
            src_ref=ups[layer][0].at[h, j],
            dst_ref=ups[layer][1].at[h, j],
            send_sem=up_send.at[layer, h, j],
            recv_sem=up_recv.at[layer, h, j],
            device_id=(row, col + 2),
            device_id_type=MESH,
        )

    def down_copy(layer, h, j):
        return pltpu.make_async_remote_copy(
            src_ref=downs[layer][0].at[h, j],
            dst_ref=downs[layer][1].at[h, j],
            send_sem=down_send.at[layer, h, j],
            recv_sem=down_recv.at[layer, h, j],
            device_id=(row, col - 2),
            device_id_type=MESH,
        )

    def pair_sum(layer, h, d):
        pair_copy(layer, h, d).wait_recv()
        return own[h, d] + pair_in[layer, h, d]

    def send_up(layer, h, j, first):
        d = n_chip - 1 - j

        @pl.when(d > chip)
        def _():
            value = pair_sum(layer, h, d)
            if not first:
                up_copy(layer, h, j).wait_recv()
                value = value + ups[layer][1][h, j].astype(jnp.float32)
            ups[layer][0][h, j] = value.astype(LINK_TYPES[layer])
            up_copy(layer, h, j).start()

    def send_down(layer, h, j, first):
        d = j

        @pl.when(d < chip)
        def _():
            value = pair_sum(layer, h, d)
            if not first:
                down_copy(layer, h, j).wait_recv()
                value = value + downs[layer][1][h, j].astype(jnp.float32)
            downs[layer][0][h, j] = value.astype(LINK_TYPES[layer])
            down_copy(layer, h, j).start()

    def start_gather(layer, source):
        for h in range(PARTS):
            for step in range(1, n_row):
                gather_copy(layer, source, h, step).start()
        for h in range(PARTS):
            inputs[layer, h, pl.ds(pl.multiple_of(row * piece, piece), piece), :] = source[
                :, h * part : (h + 1) * part
            ]

    def chunk(layer, h, index):
        rows = pl.ds(pl.multiple_of(index * piece, piece), piece)
        return jnp.dot(dense[rows, :], inputs[layer, h], preferred_element_type=jnp.float32)

    def aggregate(layer, source):
        for h in range(PARTS):
            for step in range(1, n_row):
                gather_copy(layer, source, h, step).wait_recv()

            def one_chunk(i, carry):
                d = jnp.where(i % 2 == 0, n_chip - 1 - i // 2, i // 2)
                pair_out[layer, h, d] = chunk(layer, h, d * 2 + (1 - core))
                pair_copy(layer, h, d).start()
                own[h, d] = chunk(layer, h, d * 2 + core)
                return carry

            lax.fori_loop(0, n_chip, one_chunk, 0)

            @pl.when(chip == 0)
            def _():
                lax.fori_loop(0, n_chip - 1, lambda j, c: (send_up(layer, h, j, True), c)[1], 0)

            @pl.when(chip == n_chip - 1)
            def _():
                lax.fori_loop(0, n_chip - 1, lambda j, c: (send_down(layer, h, j, True), c)[1], 0)

        for h in range(PARTS):

            def forward(j, carry):
                @pl.when(chip > 0)
                def _():
                    send_up(layer, h, j, False)

                @pl.when(chip < n_chip - 1)
                def _():
                    send_down(layer, h, j, False)

                return carry

            lax.fori_loop(0, n_chip - 1, forward, 0)
        for h in range(PARTS):
            columns = slice(h * part, (h + 1) * part)
            total[:, columns] = pair_sum(layer, h, chip)

            @pl.when(chip > 0)
            def _():
                j = n_chip - 1 - chip
                up_copy(layer, h, j).wait_recv()
                total[:, columns] += ups[layer][1][h, j].astype(jnp.float32)

            @pl.when(chip < n_chip - 1)
            def _():
                down_copy(layer, h, chip).wait_recv()
                total[:, columns] += downs[layer][1][h, chip].astype(jnp.float32)

    def project(layer):
        product = jnp.dot(
            total[...], weights[layer], precision=lax.Precision.HIGHEST,
            preferred_element_type=jnp.float32,
        )
        return jnp.maximum(product, 0.0)

    start_gather(0, features_ref)
    tiles[slots] = jnp.zeros((tile, tile), tiles.dtype)
    tile_load.wait()

    def place_row(i, carry):
        rows = pl.ds(pl.multiple_of(i * tile, tile), tile)
        for t in range(tile_cols):
            slot = inverse_ref[i * tile_cols + t]
            dense[rows, t * tile : (t + 1) * tile] = tiles[slot]
        return carry

    lax.fori_loop(0, tile_rows, place_row, 0)
    for load in weight_loads:
        load.wait()

    aggregate(0, features_ref)
    hidden[...] = project(0).astype(hidden.dtype)
    start_gather(1, hidden)
    aggregate(1, hidden)
    out_ref[...] = project(1)

    for layer, source in enumerate((features_ref, hidden)):
        for h in range(PARTS):
            for step in range(1, n_row):
                gather_copy(layer, source, h, step).wait_send()

            def drain_pair(d, carry):
                pair_copy(layer, h, d).wait_send()
                return carry

            lax.fori_loop(0, n_chip, drain_pair, 0)

            def drain(j, carry):
                @pl.when(n_chip - 1 - j > chip)
                def _():
                    up_copy(layer, h, j).wait_send()

                @pl.when(j < chip)
                def _():
                    down_copy(layer, h, j).wait_send()

                return carry

            lax.fori_loop(0, n_chip - 1, drain, 0)


def shards(n_row, n_col, features, tile_values, tile_places, tile_counts, weight_one, weight_two):
    tiles = tile_values.reshape(tile_values.shape[2:])
    places = tile_places.reshape(tile_places.shape[2:])
    slots, tile = tiles.shape[0], tiles.shape[1]
    piece, width = features.shape
    part = width // PARTS
    rows, depth = piece * n_col, piece * n_row
    tile_rows, tile_cols = rows // tile, depth // tile
    n_chip = n_col // 2
    count = tile_counts[lax.axis_index("row"), lax.axis_index("col")]
    order = jnp.arange(slots, dtype=jnp.int32)
    position = jnp.where(order < count, places[0] * tile_cols + places[1], -1)
    spots = jnp.arange(tile_rows * tile_cols, dtype=jnp.int32)
    inverse = slots + jnp.sum(
        jnp.where(position[None, :] == spots[:, None], order[None, :] - slots, 0), axis=1
    )

    def flow(layer):
        return pltpu.VMEM((PARTS, n_chip - 1, piece, part), LINK_TYPES[layer])

    dma = pltpu.SemaphoreType.DMA
    any_space = pl.BlockSpec(memory_space=pl.ANY)
    vmem = pl.BlockSpec(memory_space=pltpu.VMEM)
    return pl.pallas_call(
        functools.partial(kernel, n_row, n_col),
        out_shape=jax.ShapeDtypeStruct((piece, width), jnp.float32),
        in_specs=[pl.BlockSpec(memory_space=pltpu.SMEM), vmem, any_space, any_space, any_space],
        out_specs=vmem,
        scratch_shapes=[
            pltpu.VMEM((slots + 1, tile, tile), jnp.bfloat16),
            pltpu.VMEM((rows, depth), jnp.bfloat16),
            pltpu.VMEM((2, width, width), jnp.float32),
            pltpu.VMEM((piece, width), jnp.bfloat16),
            pltpu.VMEM((2, PARTS, depth, part), jnp.bfloat16),
            pltpu.VMEM((PARTS, n_chip, piece, part), jnp.float32),
            pltpu.VMEM((piece, width), jnp.float32),
            pltpu.VMEM((2, PARTS, n_chip, piece, part), jnp.float32),
            pltpu.VMEM((2, PARTS, n_chip, piece, part), jnp.float32),
            flow(0), flow(0), flow(0), flow(0), flow(1), flow(1), flow(1), flow(1),
            dma((3,)),
            dma((2, PARTS, n_row - 1)), dma((2, PARTS, n_row - 1)),
            dma((2, PARTS, n_chip)), dma((2, PARTS, n_chip)),
            dma((2, PARTS, n_chip - 1)), dma((2, PARTS, n_chip - 1)),
            dma((2, PARTS, n_chip - 1)), dma((2, PARTS, n_chip - 1)),
        ],
        compiler_params=pltpu.CompilerParams(
            collective_id=0, has_side_effects=True, vmem_limit_bytes=60 * 1024 * 1024
        ),
    )(inverse, features, tiles, weight_one, weight_two)


def solution(mesh):
    placed = (
        P(("row", "col"), None),
        P("row", "col", None, None, None),
        P("row", "col", None, None),
        P(),
        P(),
        P(),
    )
    return jax.shard_map(
        functools.partial(shards, mesh.shape["row"], mesh.shape["col"]),
        mesh=mesh, in_specs=placed, out_specs=P(("row", "col"), None), check_vma=False,
    )
```

time: 432 us -> 106 us (0.25)
  waiting for transfers between devices: 250 us -> 0 us
  Pallas kernels: 0 us -> 101 us
  other arithmetic: 97 us -> 2.03 us
  matrix products: 42.7 us -> 0 us
  local copies, waits for them, and re-layouts: 26.2 us -> 3.13 us
  between operations: 13.9 us -> 0.02 us
    reduce_scatter x2 -> x0, waiting for transfers between devices: 196 us -> none  [layer(): lax.psum_scatter(partial_value.reshape(TR * tile_size, width_all), 'col',...]
    pallas_call x0 -> x1, Pallas kernels: none -> 101 us  [shards(): pl.pallas_call(functools.partial(kernel, n_row, n_col), out_shape=jax.Sha...]
    scatter-add x10 -> x0, other arithmetic: 89.2 us -> none  [one_turn(): return totals.at[local_rows].add(products)]
    all_gather x2 -> x0, waiting for transfers between devices: 53.4 us -> none  [layer(): gathered = lax.all_gather(inputs, 'row', axis=0, tiled=True)]
    dot_general x12 -> x0, matrix products: 42.7 us -> none  [the longest x10 37.1 us: one_turn(): jnp.einsum('sij,sjf->sif', tile_group, column_tiles[group_cols], preferre...]
    gather x10 -> x0, local copies, waits for them, and re-layouts: 19.1 us -> none  [one_turn(): column_tiles[group_cols]]
    and x10 -> x0, other arithmetic: 6.94 us -> none  [one_turn(): (positions >= jnp.maximum(first_slot, group * group_size)) & (positions <...]
    another operation x2 -> x0, local copies, waits for them, and re-layouts: 4.99 us -> none
  transfers between devices with their start and end apart: 4 -> 0, of which waited for: 4 -> 0; matrix products, arithmetic and copies ran while one was open for 0% -> 0% of each run, Pallas kernels for 0% -> 0%
where the time goes in v1:
time: 106 us
  Pallas kernels  101 us (95%)
  local copies, waits for them, and re-layouts  3.13 us (3%)
  other arithmetic  2.03 us (2%)
    pallas_call x1, Pallas kernels, shards(): pl.pallas_call(functools.partial(kernel, n_row, n_col), out_shape=jax.Sha...  101 us

profile of v1, /device:TPU:0, one launch (start us, length us, event | category | flops | bytes accessed | tf_op | source)
XLA Modules:
  0.0 106.1 jit_solution(11802275556406544627)
XLA Ops:
  0.0 1.3 %dynamic_slice.3 = s32[1,1]{1,0:T(1,128)} dynamic-slice(s32[4,8]{1,0:T(4,128)} %param.9, s32[]{:T(128)S(6)} %select_n.18, s32[]{:T(128)S(6)} %select_n.19), dynamic_slice_sizes={1,1} | dynamic-slice | bytes 12 | tf_op jit(solution)/shard_map/dynamic_slice | solution.py:256
  1.3 1.4 %compare_select_fusion = (s32[128]{0:T(128)S(1)}, s32[128]{0:T(128)S(1)}) fusion(s32[1,1,2,128]{3,2,1,0:T(2,128)} %param.8, s32[]{:T(128)} %bitcast), kind=kLoop, calls=%fused_computation.2 | loop fusion | flops 640 | bytes 2052 | tf_op jit(solution)/shard_map/jit(_where)/select_n | solution.py:258
  2.7 0.1 select_reduce_fusion
  2.8 0.5 broadcast_add_fusion.inverse_ref
  3.3 100.9 %shard_map.64 = f32[256,512]{1,0:T(8,128)} custom-call(s32[128]{0:T(128)} %broadcast_add_fusion.inverse_ref, bf16[256,512]{1,0:T(8,128)(2,1)} %features_ref.1, bf16[128,128,128]{2,1,0:T(8,128)(2,1)} %bitcast.4, f32[512,512]{1,0:T(8,128)} %weight_one_hbm.1, f32[512,512]{1,0:T(8,128)} %weight_two_hbm.1), custom_call_target="tpu_custom_call" | custom-call | tf_op jit(solution)/shard_map/pallas_call | solution.py:270
  104.2 1.9 %copy.8 = f32[256,512]{1,0:T(8,128)} copy(f32[256,512]{1,0:T(8,128)} %shard_map.64) | data formatting | bytes 1048576

commit v2 on v1

--- a/solution.py
+++ b/solution.py
@@ -8,17 +8,22 @@
 from jax.sharding import PartitionSpec as P
 
 MESH = pl.DeviceIdType.MESH
-PARTS = 2
-LINK_TYPES = (jnp.float32, jnp.bfloat16)
+PARTS = 4
+LINK_TYPES = (jnp.int16, jnp.bfloat16)
+TOP = 32766.0
+SKEW = 2
 
 
 def kernel(
     n_row, n_col,
-    inverse_ref, features_ref, tiles_hbm, weight_one_hbm, weight_two_hbm,
+    counts_ref, places_ref, features_ref, tiles_hbm, weight_one_hbm, weight_two_hbm,
     out_ref,
     tiles, dense, weights, hidden, inputs, own, total,
     pair_out, pair_in, up_out0, up_in0, down_out0, down_in0, up_out1, up_in1, down_out1, down_in1,
+    scale_up_out, scale_up_in, scale_down_out, scale_down_in,
     load_sem, gather_send, gather_recv, pair_send, pair_recv, up_send, up_recv, down_send, down_recv,
+    scale_send, scale_recv,
+    inverse_rows, inverse_ref,
 ):
     row, col = lax.axis_index("row"), lax.axis_index("col")
     n_chip = n_col // 2
@@ -99,6 +104,45 @@
             device_id_type=MESH,
         )
 
+    scales = ((scale_up_out, scale_up_in), (scale_down_out, scale_down_in))
+
+    def scale_copy(way, h, j):
+        return pltpu.make_async_remote_copy(
+            src_ref=scales[way][0].at[h, j],
+            dst_ref=scales[way][1].at[h, j],
+            send_sem=scale_send.at[way, h, j],
+            recv_sem=scale_recv.at[way, h, j],
+            device_id=(row, col + 2 if way == 0 else col - 2),
+            device_id_type=MESH,
+        )
+
+    def flow_copy(layer, way, h, j):
+        return (up_copy, down_copy)[way](layer, h, j)
+
+    def flow_send(layer, way, h, j, value):
+        target = (ups, downs)[way][layer][0]
+        if LINK_TYPES[layer] == jnp.int16:
+            peak = jnp.maximum(jnp.max(jnp.abs(value), axis=0, keepdims=True), 1e-30)
+            scales[way][0][h, j] = jnp.broadcast_to(peak * (1.0 / TOP), scales[way][0].shape[2:])
+            scale_copy(way, h, j).start()
+            target[h, j] = jnp.round(value * (TOP / peak)).astype(jnp.int32).astype(jnp.int16)
+        else:
+            target[h, j] = value.astype(target.dtype)
+        flow_copy(layer, way, h, j).start()
+
+    def flow_take(layer, way, h, j):
+        source = (ups, downs)[way][layer][1]
+        flow_copy(layer, way, h, j).wait_recv()
+        if LINK_TYPES[layer] == jnp.int16:
+            scale_copy(way, h, j).wait_recv()
+            return source[h, j].astype(jnp.int32).astype(jnp.float32) * scales[way][1][h, j, 0:1, :]
+        return source[h, j].astype(jnp.float32)
+
+    def flow_drain(layer, way, h, j):
+        flow_copy(layer, way, h, j).wait_send()
+        if LINK_TYPES[layer] == jnp.int16:
+            scale_copy(way, h, j).wait_send()
+
     def pair_sum(layer, h, d):
         pair_copy(layer, h, d).wait_recv()
         return own[h, d] + pair_in[layer, h, d]
@@ -110,10 +154,8 @@
         def _():
             value = pair_sum(layer, h, d)
             if not first:
-                up_copy(layer, h, j).wait_recv()
-                value = value + ups[layer][1][h, j].astype(jnp.float32)
-            ups[layer][0][h, j] = value.astype(LINK_TYPES[layer])
-            up_copy(layer, h, j).start()
+                value = value + flow_take(layer, 0, h, j)
+            flow_send(layer, 0, h, j, value)
 
     def send_down(layer, h, j, first):
         d = j
@@ -122,10 +164,8 @@
         def _():
             value = pair_sum(layer, h, d)
             if not first:
-                down_copy(layer, h, j).wait_recv()
-                value = value + downs[layer][1][h, j].astype(jnp.float32)
-            downs[layer][0][h, j] = value.astype(LINK_TYPES[layer])
-            down_copy(layer, h, j).start()
+                value = value + flow_take(layer, 1, h, j)
+            flow_send(layer, 1, h, j, value)
 
     def start_gather(layer, source):
         for h in range(PARTS):
@@ -141,6 +181,19 @@
         return jnp.dot(dense[rows, :], inputs[layer, h], preferred_element_type=jnp.float32)
 
     def aggregate(layer, source):
+        turns = n_chip - 1
+        steps = PARTS * turns
+
+        def forward(time, carry):
+            for send, hops in ((send_up, chip), (send_down, turns - chip)):
+                step = time - SKEW * hops
+
+                @pl.when((step >= 0) & (step < steps) & (hops > 0))
+                def _():
+                    send(layer, step // turns, step % turns, False)
+
+            return carry
+
         for h in range(PARTS):
             for step in range(1, n_row):
                 gather_copy(layer, source, h, step).wait_recv()
@@ -162,50 +215,47 @@
             def _():
                 lax.fori_loop(0, n_chip - 1, lambda j, c: (send_down(layer, h, j, True), c)[1], 0)
 
-        for h in range(PARTS):
-
-            def forward(j, carry):
-                @pl.when(chip > 0)
-                def _():
-                    send_up(layer, h, j, False)
-
-                @pl.when(chip < n_chip - 1)
-                def _():
-                    send_down(layer, h, j, False)
-
-                return carry
-
-            lax.fori_loop(0, n_chip - 1, forward, 0)
+            lax.fori_loop(h * turns, (h + 1) * turns, forward, 0)
+
+        lax.fori_loop(steps, steps + SKEW * turns, forward, 0)
         for h in range(PARTS):
             columns = slice(h * part, (h + 1) * part)
             total[:, columns] = pair_sum(layer, h, chip)
 
             @pl.when(chip > 0)
             def _():
-                j = n_chip - 1 - chip
-                up_copy(layer, h, j).wait_recv()
-                total[:, columns] += ups[layer][1][h, j].astype(jnp.float32)
+                total[:, columns] += flow_take(layer, 0, h, n_chip - 1 - chip)
 
             @pl.when(chip < n_chip - 1)
             def _():
-                down_copy(layer, h, chip).wait_recv()
-                total[:, columns] += downs[layer][1][h, chip].astype(jnp.float32)
+                total[:, columns] += flow_take(layer, 1, h, chip)
 
     def project(layer):
-        product = jnp.dot(
+        return jnp.dot(
             total[...], weights[layer], precision=lax.Precision.HIGHEST,
             preferred_element_type=jnp.float32,
         )
-        return jnp.maximum(product, 0.0)
 
     start_gather(0, features_ref)
     tiles[slots] = jnp.zeros((tile, tile), tiles.dtype)
+    spots = tile_rows * tile_cols
+    count = counts_ref[row, col]
+    order = lax.broadcasted_iota(jnp.int32, (spots, slots), 1)
+    spot = lax.broadcasted_iota(jnp.int32, (spots, slots), 0)
+    place = places_ref[0:1, :] * tile_cols + places_ref[1:2, :]
+    listed = (place == spot) & (order < count)
+    marks = jnp.where(listed, order - slots, 0)
+    found = jnp.sum(marks.T, axis=0, keepdims=True) + slots
+    inverse_rows[...] = jnp.broadcast_to(found, inverse_rows.shape)
+    inverse_load = pltpu.make_async_copy(inverse_rows, inverse_ref, load_sem.at[3])
+    inverse_load.start()
+    inverse_load.wait()
     tile_load.wait()
 
     def place_row(i, carry):
         rows = pl.ds(pl.multiple_of(i * tile, tile), tile)
         for t in range(tile_cols):
-            slot = inverse_ref[i * tile_cols + t]
+            slot = jnp.clip(inverse_ref[0, i * tile_cols + t], 0, slots)
             dense[rows, t * tile : (t + 1) * tile] = tiles[slot]
         return carry
 
@@ -214,7 +264,7 @@
         load.wait()
 
     aggregate(0, features_ref)
-    hidden[...] = project(0).astype(hidden.dtype)
+    hidden[...] = jnp.maximum(project(0), 0.0).astype(hidden.dtype)
     start_gather(1, hidden)
     aggregate(1, hidden)
     out_ref[...] = project(1)
@@ -233,11 +283,11 @@
             def drain(j, carry):
                 @pl.when(n_chip - 1 - j > chip)
                 def _():
-                    up_copy(layer, h, j).wait_send()
+                    flow_drain(layer, 0, h, j)
 
                 @pl.when(j < chip)
                 def _():
-                    down_copy(layer, h, j).wait_send()
+                    flow_drain(layer, 1, h, j)
 
                 return carry
 
@@ -253,24 +303,19 @@
     rows, depth = piece * n_col, piece * n_row
     tile_rows, tile_cols = rows // tile, depth // tile
     n_chip = n_col // 2
-    count = tile_counts[lax.axis_index("row"), lax.axis_index("col")]
-    order = jnp.arange(slots, dtype=jnp.int32)
-    position = jnp.where(order < count, places[0] * tile_cols + places[1], -1)
-    spots = jnp.arange(tile_rows * tile_cols, dtype=jnp.int32)
-    inverse = slots + jnp.sum(
-        jnp.where(position[None, :] == spots[:, None], order[None, :] - slots, 0), axis=1
-    )
+    spots = tile_rows * tile_cols
 
     def flow(layer):
         return pltpu.VMEM((PARTS, n_chip - 1, piece, part), LINK_TYPES[layer])
 
+    scale = pltpu.VMEM((PARTS, n_chip - 1, 8, part), jnp.float32)
     dma = pltpu.SemaphoreType.DMA
     any_space = pl.BlockSpec(memory_space=pl.ANY)
     vmem = pl.BlockSpec(memory_space=pltpu.VMEM)
-    return pl.pallas_call(
+    second = pl.pallas_call(
         functools.partial(kernel, n_row, n_col),
         out_shape=jax.ShapeDtypeStruct((piece, width), jnp.float32),
-        in_specs=[pl.BlockSpec(memory_space=pltpu.SMEM), vmem, any_space, any_space, any_space],
+        in_specs=[pl.BlockSpec(memory_space=pltpu.SMEM), vmem, vmem, any_space, any_space, any_space],
         out_specs=vmem,
         scratch_shapes=[
             pltpu.VMEM((slots + 1, tile, tile), jnp.bfloat16),
@@ -283,16 +328,20 @@
             pltpu.VMEM((2, PARTS, n_chip, piece, part), jnp.float32),
             pltpu.VMEM((2, PARTS, n_chip, piece, part), jnp.float32),
             flow(0), flow(0), flow(0), flow(0), flow(1), flow(1), flow(1), flow(1),
-            dma((3,)),
+            scale, scale, scale, scale,
+            dma((4,)),
             dma((2, PARTS, n_row - 1)), dma((2, PARTS, n_row - 1)),
             dma((2, PARTS, n_chip)), dma((2, PARTS, n_chip)),
             dma((2, PARTS, n_chip - 1)), dma((2, PARTS, n_chip - 1)),
             dma((2, PARTS, n_chip - 1)), dma((2, PARTS, n_chip - 1)),
+            dma((2, PARTS, n_chip - 1)), dma((2, PARTS, n_chip - 1)),
+            pltpu.VMEM((8, spots), jnp.int32), pltpu.SMEM((8, spots), jnp.int32),
         ],
         compiler_params=pltpu.CompilerParams(
             collective_id=0, has_side_effects=True, vmem_limit_bytes=60 * 1024 * 1024
         ),
-    )(inverse, features, tiles, weight_one, weight_two)
+    )(tile_counts, places, features, tiles, weight_one, weight_two)
+    return jnp.maximum(second, 0.0)
 
 
 def solution(mesh):

time: 106 us -> 76.6 us (0.72)
  Pallas kernels: 101 us -> 74.5 us
  local copies, waits for them, and re-layouts: 3.13 us -> 0 us
    pallas_call x1, Pallas kernels: 101 us -> 74.5 us  [shards(): pl.pallas_call(functools.partial(kernel, n_row, n_col), out_shape=jax.Sha...]
    max x0 -> x1, other arithmetic: none -> 1.88 us  [shards(): return jnp.maximum(second, 0.0)]
    unnamed x1 -> x0, local copies, waits for them, and re-layouts: 1.87 us -> none
    select_n x1 -> x0, other arithmetic: 1.4 us -> none  [shards(): position = jnp.where(order < count, places[0] * tile_cols + places[1], -1)]
    dynamic_slice x1 -> x0, local copies, waits for them, and re-layouts: 1.26 us -> none  [shards(): count = tile_counts[lax.axis_index('row'), lax.axis_index('col')]]
where the time goes in v2:
time: 76.6 us; the launch traced here: 76.4 us
  Pallas kernels  74.5 us (97%)
  other arithmetic  1.88 us (2%)
    pallas_call x1, Pallas kernels, shards(): pl.pallas_call(functools.partial(kernel, n_row, n_col), out_shape=jax.Sha...  74.5 us
    max x1, other arithmetic, shards(): return jnp.maximum(second, 0.0)  1.88 us

profile of v2, /device:TPU:0, one launch (start us, length us, event | category | flops | bytes accessed | tf_op | source)
XLA Modules:
  0.0 76.4 jit_solution(17292808601533919245)
XLA Ops:
  0.0 74.5 %shard_map.64 = f32[256,512]{1,0:T(8,128)} custom-call(s32[4,8]{1,0:T(4,128)} %counts_ref.1, s32[2,128]{1,0:T(2,128)} %bitcast.3, bf16[256,512]{1,0:T(8,128)(2,1)} %features_ref.1, bf16[128,128,128]{2,1,0:T(8,128)(2,1)} %bitcast.2, f32[512,512]{1,0:T(8,128)} %weight_one_hbm.1, f32[512,512]{1,0:T(8,128)} %weight_two_hbm.1), custom_call_target="tpu_custom_call" | custom-call | tf_op jit(solution)/shard_map/pallas_call | solution.py:315
  74.6 1.9 %broadcast_maximum_fusion = f32[256,512]{1,0:T(8,128)} fusion(f32[256,512]{1,0:T(8,128)} %shard_map.64), kind=kLoop, calls=%fused_computation | loop fusion | flops 131072 | bytes 1048576 | tf_op jit(solution)/shard_map/max | solution.py:344
